TPU v7x, 32 devices: a whole 2x2x4 slice. The times are simulated.
32 devices in a mesh: row: 8 (over y, x, core), col: 4 (over z).
Axes of the slice: x: 2, y: 2, z: 4, core: 2. Of those that a mesh axis runs over, the one named last changes fastest.
Arguments:
- tokens: bfloat16 [32, 8192], P(None, 'row'), may hold values from -6 to 6
- gain: float32 [8192], P('row'), may hold values from 0.24 to 4.5
- gate_weight: bfloat16 [8192, 28672], P('row', 'col'), may hold values from -0.0625 to 0.0625
- up_weight: bfloat16 [8192, 28672], P('row', 'col'), may hold values from -0.0625 to 0.0625
- down_weight: bfloat16 [28672, 8192], P('col', 'row'), may hold values from -0.03125 to 0.03125
- probes: float32 [4, 32, 8192], P(None, None, 'row'), may hold values from -6 to 6
Outputs:
- basis: float32 [4, 32, 8192], P(None, None, 'row')
- stretch: float32 [4], replicated
All inputs are finite; a program needn't handle non-finite values.
Results may differ from a plain program's by a relative error of at most 0.0085.
Values may be sent and summed in bfloat16 or wider, within the bound.
No kernel may reach another device: no remote copies, remote signals or barrier semaphores. Data moves between devices by JAX's collectives and lax.ppermute only.
A program may use at most 128 MiB of HBM per device.

v0:
```python
import jax
import jax.numpy as jnp
from jax import lax
from jax.sharding import PartitionSpec as P

ITERS = 3
epsilon = 1e-06


def local(tokens, gain, gate_weight, up_weight, down_weight, probes):
    scaled = (tokens.astype(jnp.float32) * gain).astype(jnp.bfloat16)
    gate_part = jnp.dot(scaled, gate_weight, preferred_element_type=jnp.float32)
    up_part = jnp.dot(scaled, up_weight, preferred_element_type=jnp.float32)
    gate, up = lax.psum((gate_part, up_part), "row")
    sigmoid_gate = 1.0 / (1.0 + jnp.exp(-gate))
    activated = gate * sigmoid_gate
    slope = sigmoid_gate * (1.0 + gate * (1.0 - sigmoid_gate)) * up
    probe_count, token_count, local_width = probes.shape
    row_count = probe_count * token_count
    slope_all = jnp.tile(slope, (probe_count, 1))
    activated_all = jnp.tile(activated, (probe_count, 1))
    entries = token_count * local_width * lax.axis_size("row")
    transposed = (((1,), (1,)), ((), ()))
    current = probes
    level = jnp.zeros((probe_count,), jnp.float32)
    for sweep in range(ITERS):
        pushed = (current * gain).astype(jnp.bfloat16).reshape(row_count, local_width)
        gate_tan = jnp.dot(pushed, gate_weight, preferred_element_type=jnp.float32)
        up_tan = jnp.dot(pushed, up_weight, preferred_element_type=jnp.float32)
        joined = slope_all * gate_tan + activated_all * up_tan
        hidden = lax.psum_scatter(joined, "row", scatter_dimension=0, tiled=True).astype(
            jnp.bfloat16
        )
        tangent_part = jnp.dot(
            lax.all_gather(hidden, "row", axis=0, tiled=True),
            down_weight,
            preferred_element_type=jnp.float32,
        )
        tangent = lax.psum(tangent_part, "col").astype(jnp.bfloat16)
        back_part = lax.dot_general(
            tangent, down_weight, transposed, preferred_element_type=jnp.float32
        )
        back = lax.psum(back_part, "row").astype(jnp.bfloat16)
        gate_pull = (slope_all * back).astype(jnp.bfloat16)
        up_pull = (activated_all * back).astype(jnp.bfloat16)
        result = lax.dot_general(
            gate_pull, gate_weight, transposed, preferred_element_type=jnp.float32
        )
        pulled_part = result + lax.dot_general(
            up_pull, up_weight, transposed, preferred_element_type=jnp.float32
        )
        pulled = lax.psum(pulled_part, "col")
        grown = pulled.reshape(probe_count, token_count, local_width) * gain
        squares = jnp.sum(grown * grown, axis=(1, 2))
        level = lax.psum(squares, "row") / entries
        current = grown * lax.rsqrt(level + epsilon)[:, None, None]
    return (current, jnp.sqrt(level))


def solution(mesh):
    placed = (
        P(None, "row"),
        P("row"),
        P("row", "col"),
        P("row", "col"),
        P("col", "row"),
        P(None, None, "row"),
    )
    return jax.shard_map(
        local, mesh=mesh, in_specs=placed, out_specs=(P(None, None, "row"), P()), check_vma=False
    )
```

profile of v0, /device:TPU:0, one launch (start us, length us, event | category | flops | bytes accessed | tf_op | source)
XLA Modules:
  0.0 980.3 jit_solution(12763348402583226516)
XLA Ops:
  7.2 8.9 fusion.16
  16.2 0.8 copy-done
  17.0 3.6 fusion.17
  20.7 63.1 %all-reduce.18.cloned.1.call-done = (f32[32,7168]{1,0:T(8,128)}, f32[32,7168]{1,0:T(8,128)}) async-done(((f32[32,7168]{1,0:T(8,128)}, f32[32,7168]{1,0:T(8,128)}), (f32[32,7168]{1,0:T(8,128)}, f32[32,7168]{1,0:T(8,128)})) %all-reduce.18.cloned.1.call-update) | async-done | bytes 1835024 | tf_op jit(solution)/shard_map/psum | solution.py:14
  83.7 1.8 fusion.9
  85.6 7.3 bitcast_multiply_fusion.5
  92.8 9.3 fusion
  102.2 47.9 %reduce-scatter.4.cloned.1.call-done = f32[16,7168]{1,0:T(8,128)} async-done(((f32[128,7168]{1,0:T(8,128)}), f32[16,7168]{1,0:T(8,128)}) %reduce-scatter.4.cloned.1.call-update) | async-done | bytes 458768 | tf_op jit(solution)/shard_map/reduce_scatter | solution.py:31
  150.1 1.7 convert_element_type.77
  151.9 27.4 %all-gather.4.cloned.1.call-done = bf16[128,7168]{1,0:T(8,128)(2,1)} async-done(((bf16[16,7168]{1,0:T(8,128)(2,1)}), bf16[128,7168]{1,0:T(8,128)(2,1)}) %all-gather.4.cloned.1.call-update) | async-done | bytes 1835024 | tf_op jit(solution)/shard_map/all_gather | solution.py:35
  179.3 7.8 fusion.18
  187.1 30.6 %all-reduce.19 = bf16[128,1024]{1,0:T(8,128)(2,1)S(1)} all-reduce(f32[128,1024]{1,0:T(8,128)S(1)} %fusion.18), channel_id=1, replica_groups=mesh['row'=8,'col'=4] {'col'}, use_global_device_ids=true, to_apply=%region_3.0 | all-reduce | flops 131072 | bytes 786432 | tf_op jit(solution)/shard_map/psum | solution.py:39
  217.7 11.8 %fusion.26 = f32[128,7168]{1,0:T(8,128)} fusion(bf16[128,1024]{1,0:T(8,128)(2,1)S(1)} %all-reduce.19, bf16[7168,1024]{1,0:T(8,128)(2,1)} %param.10), kind=kOutput, calls=%fused_computation.55 | convolution fusion | flops 1879048192 | bytes 18612224 | tf_op jit(solution)/shard_map/dot_general | solution.py:40
  229.5 77.7 %all-reduce.20 = bf16[128,7168]{1,0:T(8,128)(2,1)} all-reduce(f32[128,7168]{1,0:T(8,128)} %fusion.26), channel_id=1, replica_groups=mesh['row'=8,'col'=4] {'row'}, use_global_device_ids=true, to_apply=%region_4.0 | all-reduce | flops 917504 | bytes 5505024 | tf_op jit(solution)/shard_map/psum | solution.py:43
  307.2 2.1 fusion.6
  309.4 10.1 %fusion.19 = f32[128,1024]{1,0:T(8,128)S(1)} fusion(bf16[128,7168]{1,0:T(8,128)(2,1)S(1)} %get-tuple-element.9, bf16[1024,7168]{1,0:T(8,128)(2,1)} %param.8), kind=kOutput, calls=%fused_computation.48 | convolution fusion | flops 1879048192 | bytes 17039360 | tf_op jit(solution)/shard_map/dot_general | solution.py:46
  319.5 10.9 %convolution_add_fusion.2 = f32[128,1024]{1,0:T(8,128)} fusion(f32[128,1024]{1,0:T(8,128)S(1)} %fusion.19, bf16[128,7168]{1,0:T(8,128)(2,1)S(1)} %get-tuple-element.8, bf16[1024,7168]{1,0:T(8,128)(2,1)} %param.9), kind=kOutput, calls=%fused_computation.23 | convolution fusion | flops 1879179264 | bytes 17563648 | tf_op jit(solution)/shard_map/dot_general | solution.py:49
  330.4 0.0 reduce-scatter.6.cloned.1.call-start
  330.5 36.4 %all-reduce.12.cloned.1.call-done = f32[128,1024]{1,0:T(8,128)} async-done(((f32[128,1024]{1,0:T(8,128)}), f32[128,1024]{1,0:T(8,128)}) %all-reduce.12.cloned.1.call-update) | async-done | bytes 524304 | tf_op jit(solution)/shard_map/psum | solution.py:52
  366.9 1.2 multiply_reduce_fusion.2
  368.1 0.1 reduce_sum.37
  368.2 0.1 reduce_sum.38
  368.3 13.1 %psum.103 = f32[4]{0:T(128)S(1)} all-reduce(f32[4]{0:T(128)S(1)} %reduce_sum.38), channel_id=1, replica_groups=mesh['row'=8,'col'=4] {'row'}, use_global_device_ids=true, to_apply=%region_8.0 | all-reduce | flops 4 | bytes 32 | tf_op jit(solution)/shard_map/psum | solution.py:55
  381.4 0.1 mul.166
  381.5 0.1 mul.167
  381.6 7.5 bitcast_multiply_fusion.3
  389.1 9.3 fusion.1
  398.5 0.0 all-gather.6.cloned.1.call-start
  398.5 46.7 %reduce-scatter.6.cloned.1.call-done = f32[16,7168]{1,0:T(8,128)} async-done(((f32[128,7168]{1,0:T(8,128)}), f32[16,7168]{1,0:T(8,128)}) %reduce-scatter.6.cloned.1.call-update) | async-done | bytes 458768 | tf_op jit(solution)/shard_map/reduce_scatter | solution.py:31
  445.2 1.7 convert_element_type.84
  447.0 27.2 %all-gather.6.cloned.1.call-done = bf16[128,7168]{1,0:T(8,128)(2,1)} async-done(((bf16[16,7168]{1,0:T(8,128)(2,1)}), bf16[128,7168]{1,0:T(8,128)(2,1)}) %all-gather.6.cloned.1.call-update) | async-done | bytes 1835024 | tf_op jit(solution)/shard_map/all_gather | solution.py:35
  474.3 7.8 fusion.20
  482.1 30.4 %all-reduce.21 = bf16[128,1024]{1,0:T(8,128)(2,1)S(1)} all-reduce(f32[128,1024]{1,0:T(8,128)S(1)} %fusion.20), channel_id=1, replica_groups=mesh['row'=8,'col'=4] {'col'}, use_global_device_ids=true, to_apply=%region_10.0 | all-reduce | flops 131072 | bytes 786432 | tf_op jit(solution)/shard_map/psum | solution.py:39
  512.4 11.8 %fusion.25 = f32[128,7168]{1,0:T(8,128)} fusion(bf16[128,1024]{1,0:T(8,128)(2,1)S(1)} %all-reduce.21, bf16[7168,1024]{1,0:T(8,128)(2,1)} %param.10), kind=kOutput, calls=%fused_computation.54 | convolution fusion | flops 1879048192 | bytes 18612224 | tf_op jit(solution)/shard_map/dot_general | solution.py:40
  524.3 77.9 %all-reduce.22 = bf16[128,7168]{1,0:T(8,128)(2,1)} all-reduce(f32[128,7168]{1,0:T(8,128)} %fusion.25), channel_id=1, replica_groups=mesh['row'=8,'col'=4] {'row'}, use_global_device_ids=true, to_apply=%region_11.0 | all-reduce | flops 917504 | bytes 5505024 | tf_op jit(solution)/shard_map/psum | solution.py:43
  602.2 2.1 fusion.7
  604.3 10.1 %fusion.21 = f32[128,1024]{1,0:T(8,128)S(1)} fusion(bf16[128,7168]{1,0:T(8,128)(2,1)S(1)} %get-tuple-element.7, bf16[1024,7168]{1,0:T(8,128)(2,1)} %param.8), kind=kOutput, calls=%fused_computation.50 | convolution fusion | flops 1879048192 | bytes 17039360 | tf_op jit(solution)/shard_map/dot_general | solution.py:46
  614.4 10.9 %convolution_add_fusion.1 = f32[128,1024]{1,0:T(8,128)} fusion(f32[128,1024]{1,0:T(8,128)S(1)} %fusion.21, bf16[128,7168]{1,0:T(8,128)(2,1)S(1)} %get-tuple-element.6, bf16[1024,7168]{1,0:T(8,128)(2,1)} %param.9), kind=kOutput, calls=%fused_computation.22 | convolution fusion | flops 1879179264 | bytes 17563648 | tf_op jit(solution)/shard_map/dot_general | solution.py:49
  625.4 36.3 %all-reduce.14.cloned.1.call-done = f32[128,1024]{1,0:T(8,128)} async-done(((f32[128,1024]{1,0:T(8,128)}), f32[128,1024]{1,0:T(8,128)}) %all-reduce.14.cloned.1.call-update) | async-done | bytes 524304 | tf_op jit(solution)/shard_map/psum | solution.py:52
  661.7 1.2 multiply_reduce_fusion.1
  662.9 0.1 reduce_sum.40
  662.9 0.1 reduce_sum.44
  663.1 12.9 %psum.107 = f32[4]{0:T(128)S(1)} all-reduce(f32[4]{0:T(128)S(1)} %reduce_sum.44), channel_id=1, replica_groups=mesh['row'=8,'col'=4] {'row'}, use_global_device_ids=true, to_apply=%region_15.0 | all-reduce | flops 4 | bytes 32 | tf_op jit(solution)/shard_map/psum | solution.py:55
  676.0 0.1 mul.177
  676.1 0.1 mul.178
  676.2 7.5 bitcast_multiply_fusion.1
  683.7 9.3 fusion.2
  693.1 46.7 %reduce-scatter.8.cloned.1.call-done = f32[16,7168]{1,0:T(8,128)} async-done(((f32[128,7168]{1,0:T(8,128)}), f32[16,7168]{1,0:T(8,128)}) %reduce-scatter.8.cloned.1.call-update) | async-done | bytes 458768 | tf_op jit(solution)/shard_map/reduce_scatter | solution.py:31
  739.8 1.7 convert_element_type.91
  741.6 27.4 %all-gather.8.cloned.1.call-done = bf16[128,7168]{1,0:T(8,128)(2,1)} async-done(((bf16[16,7168]{1,0:T(8,128)(2,1)}), bf16[128,7168]{1,0:T(8,128)(2,1)}) %all-gather.8.cloned.1.call-update) | async-done | bytes 1835024 | tf_op jit(solution)/shard_map/all_gather | solution.py:35
  769.0 7.8 fusion.22
  776.8 30.4 %all-reduce.23 = bf16[128,1024]{1,0:T(8,128)(2,1)S(1)} all-reduce(f32[128,1024]{1,0:T(8,128)S(1)} %fusion.22), channel_id=1, replica_groups=mesh['row'=8,'col'=4] {'col'}, use_global_device_ids=true, to_apply=%region_17.0 | all-reduce | flops 131072 | bytes 786432 | tf_op jit(solution)/shard_map/psum | solution.py:39
  807.1 11.8 %fusion.24 = f32[128,7168]{1,0:T(8,128)} fusion(bf16[128,1024]{1,0:T(8,128)(2,1)S(1)} %all-reduce.23, bf16[7168,1024]{1,0:T(8,128)(2,1)} %param.10), kind=kOutput, calls=%fused_computation.53 | convolution fusion | flops 1879048192 | bytes 18612224 | tf_op jit(solution)/shard_map/dot_general | solution.py:40
  819.0 78.0 %all-reduce.24 = bf16[128,7168]{1,0:T(8,128)(2,1)} all-reduce(f32[128,7168]{1,0:T(8,128)} %fusion.24), channel_id=1, replica_groups=mesh['row'=8,'col'=4] {'row'}, use_global_device_ids=true, to_apply=%region_18.0 | all-reduce | flops 917504 | bytes 5505024 | tf_op jit(solution)/shard_map/psum | solution.py:43
  897.0 2.1 fusion.8
  899.1 10.1 %fusion.23 = f32[128,1024]{1,0:T(8,128)S(1)} fusion(bf16[128,7168]{1,0:T(8,128)(2,1)S(1)} %get-tuple-element.5, bf16[1024,7168]{1,0:T(8,128)(2,1)} %param.8), kind=kOutput, calls=%fused_computation.52 | convolution fusion | flops 1879048192 | bytes 17039360 | tf_op jit(solution)/shard_map/dot_general | solution.py:46
  909.2 10.9 %convolution_add_fusion = f32[128,1024]{1,0:T(8,128)} fusion(f32[128,1024]{1,0:T(8,128)S(1)} %fusion.23, bf16[128,7168]{1,0:T(8,128)(2,1)S(1)} %get-tuple-element.4, bf16[1024,7168]{1,0:T(8,128)(2,1)} %param.9), kind=kOutput, calls=%fused_computation.21 | convolution fusion | flops 1879179264 | bytes 17563648 | tf_op jit(solution)/shard_map/dot_general | solution.py:49
  920.2 36.3 %all-reduce.16.cloned.1.call-done = f32[128,1024]{1,0:T(8,128)} async-done(((f32[128,1024]{1,0:T(8,128)}), f32[128,1024]{1,0:T(8,128)}) %all-reduce.16.cloned.1.call-update) | async-done | bytes 524304 | tf_op jit(solution)/shard_map/psum | solution.py:52
  956.5 1.2 multiply_reduce_fusion
  957.6 0.1 reduce_sum.55
  957.7 0.1 reduce_sum.56
  957.8 12.7 %psum.111 = f32[4]{0:T(128)S(1)} all-reduce(f32[4]{0:T(128)S(1)} %reduce_sum.56), channel_id=1, replica_groups=mesh['row'=8,'col'=4] {'row'}, use_global_device_ids=true, to_apply=%region_22.23 | all-reduce | flops 4 | bytes 32 | tf_op jit(solution)/shard_map/psum | solution.py:55
  970.6 0.5 multiply_sqrt_fusion
  971.1 2.0 multiply_multiply_fusion.1
  (32 shorter events, 0.6 us)
Async XLA Ops:
  7.2 9.0 copy-start.3
  7.2 9.0 copy-start.5
  7.2 76.6 %all-reduce.18.cloned.1.call-start = ((), (), s32[]{:S(2)}) async-start(), calls=%async_computation.12 | async-start | bytes 3670016 | tf_op jit(solution)/shard_map/psum | solution.py:14
  7.2 9.7 copy-start
  17.0 3.7 copy-start.4
  20.6 129.5 %reduce-scatter.4.cloned.1.call-start = ((), (), s32[]{:S(2)}) async-start(), calls=%async_computation.3 | async-start | bytes 4128768 | tf_op jit(solution)/shard_map/reduce_scatter | solution.py:31
  102.2 77.1 %all-gather.4.cloned.1.call-start = ((), (), s32[]{:S(2)}) async-start(), calls=%async_computation.4 | async-start | bytes 2064384 | tf_op jit(solution)/shard_map/all_gather | solution.py:35
  151.8 215.0 %all-reduce.12.cloned.1.call-start = ((), (), s32[]{:S(2)}) async-start(), calls=%async_computation.5 | async-start | bytes 1048576 | tf_op jit(solution)/shard_map/psum | solution.py:52
  330.4 114.8 %reduce-scatter.6.cloned.1.call-start = ((), (), s32[]{:S(2)}) async-start(), calls=%async_computation.6 | async-start | bytes 4128768 | tf_op jit(solution)/shard_map/reduce_scatter | solution.py:31
  381.6 7.6 copy-start.1
  398.5 75.8 %all-gather.6.cloned.1.call-start = ((), (), s32[]{:S(2)}) async-start(), calls=%async_computation.7 | async-start | bytes 2064384 | tf_op jit(solution)/shard_map/all_gather | solution.py:35
  447.0 214.7 %all-reduce.14.cloned.1.call-start = ((), (), s32[]{:S(2)}) async-start(), calls=%async_computation.8 | async-start | bytes 1048576 | tf_op jit(solution)/shard_map/psum | solution.py:52
  625.4 114.4 %reduce-scatter.8.cloned.1.call-start = ((), (), s32[]{:S(2)}) async-start(), calls=%async_computation.9 | async-start | bytes 4128768 | tf_op jit(solution)/shard_map/reduce_scatter | solution.py:31
  676.2 7.6 copy-start.2
  693.1 75.9 %all-gather.8.cloned.1.call-start = ((), (), s32[]{:S(2)}) async-start(), calls=%async_computation.10 | async-start | bytes 2064384 | tf_op jit(solution)/shard_map/all_gather | solution.py:35
  741.6 214.9 %all-reduce.16.cloned.1.call-start = ((), (), s32[]{:S(2)}) async-start(), calls=%async_computation.11 | async-start | bytes 1048576 | tf_op jit(solution)/shard_map/psum | solution.py:52
Sparse Core Ops, SparseCore 0:
  20.7 63.0 all-reduce.17
  102.3 47.7 reduce-scatter.3
  152.6 26.6 all-gather.3
  330.5 36.3 all-reduce.11
  398.6 46.5 reduce-scatter.5
  447.5 26.6 all-gather.5
  625.5 36.1 all-reduce.13
  693.2 46.5 reduce-scatter.7
  742.3 26.6 all-gather.7
  920.3 36.1 all-reduce.15
where the time goes:
time: 989 us; the launch traced here: 980 us
  waiting for transfers between devices  395 us (40%)
  blocking collectives  364 us (37%)
  matrix products  185 us (19%)
  other arithmetic  19.9 us (2%)
  between operations  14.8 us (1%)
    psum x3, blocking collectives, local(): back = lax.psum(back_part, 'row').astype(jnp.bfloat16)  234 us
    reduce_scatter x3, waiting for transfers between devices, local(): lax.psum_scatter(joined, 'row', scatter_dimension=0, tiled=True)  141 us
    psum x3, waiting for transfers between devices, local(): pulled = lax.psum(pulled_part, 'col')  109 us
    psum x3, blocking collectives, local(): tangent = lax.psum(tangent_part, 'col').astype(jnp.bfloat16)  91.3 us
    all_gather x3, waiting for transfers between devices, local(): lax.all_gather(hidden, 'row', axis=0, tiled=True)  82 us
    psum x1, waiting for transfers between devices, local(): gate, up = lax.psum((gate_part, up_part), 'row')  63.1 us
    psum x3, blocking collectives, local(): level = lax.psum(squares, 'row') / entries  38.8 us
    dot_general x3, matrix products, local(): lax.dot_general(tangent, down_weight, transposed, preferred_element_type=...  35.5 us
  transfers between devices with their start and end apart: 10, of which 10 were waited for; matrix products, arithmetic and copies ran while one was open for 0% of the time, Pallas kernels for 0%

commit v1 on v0

--- a/solution.py
+++ b/solution.py
@@ -36,7 +36,7 @@
             down_weight,
             preferred_element_type=jnp.float32,
         )
-        tangent = lax.psum(tangent_part, "col").astype(jnp.bfloat16)
+        tangent = jnp.sum(lax.all_gather(tangent_part, "col"), axis=0).astype(jnp.bfloat16)
         back_part = lax.dot_general(
             tangent, down_weight, transposed, preferred_element_type=jnp.float32
         )

time: 989 us -> 1050 us (1.062)
  waiting for transfers between devices: 395 us -> 533 us
  blocking collectives: 364 us -> 274 us
    all_gather x0 -> x3, waiting for transfers between devices: none -> 137 us  [local(): lax.all_gather(tangent_part, 'col')]
    psum x3 -> x0, blocking collectives: 91.3 us -> none  [local(): tangent = lax.psum(tangent_part, 'col').astype(jnp.bfloat16)]
  transfers between devices with their start and end apart: 10 -> 13, of which waited for: 10 -> 13; matrix products, arithmetic and copies ran while one was open for 0% -> 0% of each run, Pallas kernels for 0% -> 0%
where the time goes in v1:
time: 1050 us; the launch traced here: 1040 us
  waiting for transfers between devices  533 us (51%)
  blocking collectives  274 us (26%)
  matrix products  187 us (18%)
  other arithmetic  25.3 us (2%)
  between operations  14.5 us (1%)
    psum x3, blocking collectives, local(): back = lax.psum(back_part, 'row').astype(jnp.bfloat16)  235 us
    reduce_scatter x3, waiting for transfers between devices, local(): lax.psum_scatter(joined, 'row', scatter_dimension=0, tiled=True)  141 us
    all_gather x3, waiting for transfers between devices, local(): lax.all_gather(tangent_part, 'col')  137 us
    psum x3, waiting for transfers between devices, local(): pulled = lax.psum(pulled_part, 'col')  110 us
    all_gather x3, waiting for transfers between devices, local(): lax.all_gather(hidden, 'row', axis=0, tiled=True)  82.1 us
    psum x1, waiting for transfers between devices, local(): gate, up = lax.psum((gate_part, up_part), 'row')  63.1 us
    psum x3, blocking collectives, local(): level = lax.psum(squares, 'row') / entries  38.8 us
    dot_general x3, matrix products, local(): lax.dot_general(tangent, down_weight, transposed, preferred_element_type=...  35.5 us
  transfers between devices with their start and end apart: 13, of which 13 were waited for; matrix products, arithmetic and copies ran while one was open for 0% of the time, Pallas kernels for 0%

profile of v1, /device:TPU:0, one launch (start us, length us, event | category | flops | bytes accessed | tf_op | source)
XLA Modules:
  0.0 1036.6 jit_solution(7653385656883551981)
XLA Ops:
  7.2 8.9 fusion.16
  16.2 0.8 copy-done
  17.0 3.6 fusion.17
  20.7 63.1 %all-reduce.15.cloned.1.call-done = (f32[32,7168]{1,0:T(8,128)}, f32[32,7168]{1,0:T(8,128)}) async-done(((f32[32,7168]{1,0:T(8,128)}, f32[32,7168]{1,0:T(8,128)}), (f32[32,7168]{1,0:T(8,128)}, f32[32,7168]{1,0:T(8,128)})) %all-reduce.15.cloned.1.call-update) | async-done | bytes 1835024 | tf_op jit(solution)/shard_map/psum | solution.py:14
  83.7 1.8 fusion.9
  85.6 7.3 bitcast_multiply_fusion.5
  92.8 9.3 fusion
  102.2 47.9 %reduce-scatter.4.cloned.1.call-done = f32[16,7168]{1,0:T(8,128)} async-done(((f32[128,7168]{1,0:T(8,128)}), f32[16,7168]{1,0:T(8,128)}) %reduce-scatter.4.cloned.1.call-update) | async-done | bytes 458768 | tf_op jit(solution)/shard_map/reduce_scatter | solution.py:31
  150.1 1.7 convert_element_type.77
  151.9 27.4 %all-gather.10.cloned.1.call-done = bf16[128,7168]{1,0:T(8,128)(2,1)} async-done(((bf16[16,7168]{1,0:T(8,128)(2,1)}), bf16[128,7168]{1,0:T(8,128)(2,1)}) %all-gather.10.cloned.1.call-update) | async-done | bytes 1835024 | tf_op jit(solution)/shard_map/all_gather | solution.py:35
  179.3 8.6 fusion.18
  187.9 0.3 all-reduce.9.cloned.1.call-start
  188.2 45.5 %all-gather.16.cloned.1.call-done = f32[512,1024]{1,0:T(8,128)} async-done(((f32[128,1024]{1,0:T(8,128)}), f32[512,1024]{1,0:T(8,128)}) %all-gather.16.cloned.1.call-update) | async-done | bytes 2097168 | tf_op jit(solution)/shard_map/all_gather | solution.py:39
  233.7 1.8 reduce_sum.60
  235.5 11.8 %fusion.26 = f32[128,7168]{1,0:T(8,128)} fusion(bf16[128,1024]{1,0:T(8,128)(2,1)S(1)} %reduce_sum.60, bf16[7168,1024]{1,0:T(8,128)(2,1)} %param.10), kind=kOutput, calls=%fused_computation.55 | convolution fusion | flops 1879048192 | bytes 18612224 | tf_op jit(solution)/shard_map/dot_general | solution.py:40
  247.4 78.3 %all-reduce.16 = bf16[128,7168]{1,0:T(8,128)(2,1)} all-reduce(f32[128,7168]{1,0:T(8,128)} %fusion.26), channel_id=1, replica_groups=mesh['row'=8,'col'=4] {'row'}, use_global_device_ids=true, to_apply=%region_4.0 | all-reduce | flops 917504 | bytes 5505024 | tf_op jit(solution)/shard_map/psum | solution.py:43
  325.7 2.1 fusion.6
  327.8 10.1 fusion.19
  338.0 10.9 %convolution_add_fusion.2 = f32[128,1024]{1,0:T(8,128)} fusion(f32[128,1024]{1,0:T(8,128)S(1)} %fusion.19, bf16[128,7168]{1,0:T(8,128)(2,1)S(1)} %get-tuple-element.8, bf16[1024,7168]{1,0:T(8,128)(2,1)} %param.9), kind=kOutput, calls=%fused_computation.23 | convolution fusion | flops 1879179264 | bytes 17563648 | tf_op jit(solution)/shard_map/dot_general | solution.py:49
  348.9 36.5 %all-reduce.9.cloned.1.call-done = f32[128,1024]{1,0:T(8,128)} async-done(((f32[128,1024]{1,0:T(8,128)}), f32[128,1024]{1,0:T(8,128)}) %all-reduce.9.cloned.1.call-update) | async-done | bytes 524304 | tf_op jit(solution)/shard_map/psum | solution.py:52
  385.4 1.2 multiply_reduce_fusion.2
  386.6 0.1 reduce_sum.65
  386.7 0.1 reduce_sum.78
  386.8 13.1 %psum.81 = f32[4]{0:T(128)S(1)} all-reduce(f32[4]{0:T(128)S(1)} %reduce_sum.78), channel_id=1, replica_groups=mesh['row'=8,'col'=4] {'row'}, use_global_device_ids=true, to_apply=%region_8.0 | all-reduce | flops 4 | bytes 32 | tf_op jit(solution)/shard_map/psum | solution.py:55
  400.0 0.1 mul.167
  400.1 7.5 bitcast_multiply_fusion.3
  407.7 9.3 fusion.1
  417.1 46.7 %reduce-scatter.6.cloned.1.call-done = f32[16,7168]{1,0:T(8,128)} async-done(((f32[128,7168]{1,0:T(8,128)}), f32[16,7168]{1,0:T(8,128)}) %reduce-scatter.6.cloned.1.call-update) | async-done | bytes 458768 | tf_op jit(solution)/shard_map/reduce_scatter | solution.py:31
  463.7 1.7 convert_element_type.84
  465.5 27.4 %all-gather.12.cloned.1.call-done = bf16[128,7168]{1,0:T(8,128)(2,1)} async-done(((bf16[16,7168]{1,0:T(8,128)(2,1)}), bf16[128,7168]{1,0:T(8,128)(2,1)}) %all-gather.12.cloned.1.call-update) | async-done | bytes 1835024 | tf_op jit(solution)/shard_map/all_gather | solution.py:35
  492.9 8.6 fusion.20
  501.6 45.8 %all-gather.18.cloned.1.call-done = f32[512,1024]{1,0:T(8,128)} async-done(((f32[128,1024]{1,0:T(8,128)}), f32[512,1024]{1,0:T(8,128)}) %all-gather.18.cloned.1.call-update) | async-done | bytes 2097168 | tf_op jit(solution)/shard_map/all_gather | solution.py:39
  547.3 1.8 reduce_sum.79
  549.1 11.8 %fusion.25 = f32[128,7168]{1,0:T(8,128)} fusion(bf16[128,1024]{1,0:T(8,128)(2,1)S(1)} %reduce_sum.79, bf16[7168,1024]{1,0:T(8,128)(2,1)} %param.10), kind=kOutput, calls=%fused_computation.54 | convolution fusion | flops 1879048192 | bytes 18612224 | tf_op jit(solution)/shard_map/dot_general | solution.py:40
  561.0 78.5 %all-reduce.17 = bf16[128,7168]{1,0:T(8,128)(2,1)} all-reduce(f32[128,7168]{1,0:T(8,128)} %fusion.25), channel_id=1, replica_groups=mesh['row'=8,'col'=4] {'row'}, use_global_device_ids=true, to_apply=%region_11.0 | all-reduce | flops 917504 | bytes 5505024 | tf_op jit(solution)/shard_map/psum | solution.py:43
  639.5 2.1 fusion.7
  641.6 10.1 fusion.21
  651.7 10.9 %convolution_add_fusion.1 = f32[128,1024]{1,0:T(8,128)} fusion(f32[128,1024]{1,0:T(8,128)S(1)} %fusion.21, bf16[128,7168]{1,0:T(8,128)(2,1)S(1)} %get-tuple-element.6, bf16[1024,7168]{1,0:T(8,128)(2,1)} %param.9), kind=kOutput, calls=%fused_computation.22 | convolution fusion | flops 1879179264 | bytes 17563648 | tf_op jit(solution)/shard_map/dot_general | solution.py:49
  662.7 36.5 %all-reduce.11.cloned.1.call-done = f32[128,1024]{1,0:T(8,128)} async-done(((f32[128,1024]{1,0:T(8,128)}), f32[128,1024]{1,0:T(8,128)}) %all-reduce.11.cloned.1.call-update) | async-done | bytes 524304 | tf_op jit(solution)/shard_map/psum | solution.py:52
  699.2 1.2 multiply_reduce_fusion.1
  700.4 0.1 reduce_sum.81
  700.5 0.1 reduce_sum.82
  700.6 12.9 %psum.84 = f32[4]{0:T(128)S(1)} all-reduce(f32[4]{0:T(128)S(1)} %reduce_sum.82), channel_id=1, replica_groups=mesh['row'=8,'col'=4] {'row'}, use_global_device_ids=true, to_apply=%region_15.0 | all-reduce | flops 4 | bytes 32 | tf_op jit(solution)/shard_map/psum | solution.py:55
  713.6 0.1 mul.178
  713.7 7.5 bitcast_multiply_fusion.1
  721.3 9.3 fusion.2
  730.7 46.7 %reduce-scatter.8.cloned.1.call-done = f32[16,7168]{1,0:T(8,128)} async-done(((f32[128,7168]{1,0:T(8,128)}), f32[16,7168]{1,0:T(8,128)}) %reduce-scatter.8.cloned.1.call-update) | async-done | bytes 458768 | tf_op jit(solution)/shard_map/reduce_scatter | solution.py:31
  777.3 1.7 convert_element_type.91
  779.1 27.4 %all-gather.14.cloned.1.call-done = bf16[128,7168]{1,0:T(8,128)(2,1)} async-done(((bf16[16,7168]{1,0:T(8,128)(2,1)}), bf16[128,7168]{1,0:T(8,128)(2,1)}) %all-gather.14.cloned.1.call-update) | async-done | bytes 1835024 | tf_op jit(solution)/shard_map/all_gather | solution.py:35
  806.5 8.6 fusion.22
  815.2 45.8 %all-gather.20.cloned.1.call-done = f32[512,1024]{1,0:T(8,128)} async-done(((f32[128,1024]{1,0:T(8,128)}), f32[512,1024]{1,0:T(8,128)}) %all-gather.20.cloned.1.call-update) | async-done | bytes 2097168 | tf_op jit(solution)/shard_map/all_gather | solution.py:39
  860.9 1.8 reduce_sum.83
  862.8 11.8 %fusion.24 = f32[128,7168]{1,0:T(8,128)} fusion(bf16[128,1024]{1,0:T(8,128)(2,1)S(1)} %reduce_sum.83, bf16[7168,1024]{1,0:T(8,128)(2,1)} %param.10), kind=kOutput, calls=%fused_computation.53 | convolution fusion | flops 1879048192 | bytes 18612224 | tf_op jit(solution)/shard_map/dot_general | solution.py:40
  874.6 78.6 %all-reduce.18 = bf16[128,7168]{1,0:T(8,128)(2,1)} all-reduce(f32[128,7168]{1,0:T(8,128)} %fusion.24), channel_id=1, replica_groups=mesh['row'=8,'col'=4] {'row'}, use_global_device_ids=true, to_apply=%region_18.0 | all-reduce | flops 917504 | bytes 5505024 | tf_op jit(solution)/shard_map/psum | solution.py:43
  953.2 2.1 fusion.8
  955.3 10.1 fusion.23
  965.4 10.9 %convolution_add_fusion = f32[128,1024]{1,0:T(8,128)} fusion(f32[128,1024]{1,0:T(8,128)S(1)} %fusion.23, bf16[128,7168]{1,0:T(8,128)(2,1)S(1)} %get-tuple-element.4, bf16[1024,7168]{1,0:T(8,128)(2,1)} %param.9), kind=kOutput, calls=%fused_computation.21 | convolution fusion | flops 1879179264 | bytes 17563648 | tf_op jit(solution)/shard_map/dot_general | solution.py:49
  976.4 36.7 %all-reduce.13.cloned.1.call-done = f32[128,1024]{1,0:T(8,128)} async-done(((f32[128,1024]{1,0:T(8,128)}), f32[128,1024]{1,0:T(8,128)}) %all-reduce.13.cloned.1.call-update) | async-done | bytes 524304 | tf_op jit(solution)/shard_map/psum | solution.py:52
  1013.0 1.2 multiply_reduce_fusion
  1014.2 0.1 reduce_sum.85
  1014.3 0.1 reduce_sum.86
  1014.4 12.7 %psum.87 = f32[4]{0:T(128)S(1)} all-reduce(f32[4]{0:T(128)S(1)} %reduce_sum.86), channel_id=1, replica_groups=mesh['row'=8,'col'=4] {'row'}, use_global_device_ids=true, to_apply=%region_22.23 | all-reduce | flops 4 | bytes 32 | tf_op jit(solution)/shard_map/psum | solution.py:55
  1027.1 0.5 multiply_sqrt_fusion
  1027.6 2.0 multiply_multiply_fusion.1
  (41 shorter events, 0.9 us)
Async XLA Ops:
  7.2 9.0 copy-start.3
  7.2 9.0 copy-start.5
  7.2 76.6 %all-reduce.15.cloned.1.call-start = ((), (), s32[]{:S(2)}) async-start(), calls=%async_computation.15 | async-start | bytes 3670016 | tf_op jit(solution)/shard_map/psum | solution.py:14
  7.2 9.7 copy-start
  17.0 3.7 copy-start.4
  20.6 129.5 %reduce-scatter.4.cloned.1.call-start = ((), (), s32[]{:S(2)}) async-start(), calls=%async_computation.3 | async-start | bytes 4128768 | tf_op jit(solution)/shard_map/reduce_scatter | solution.py:31
  102.2 77.1 %all-gather.10.cloned.1.call-start = ((), (), s32[]{:S(2)}) async-start(), calls=%async_computation.4 | async-start | bytes 2064384 | tf_op jit(solution)/shard_map/all_gather | solution.py:35
  151.8 81.9 %all-gather.16.cloned.1.call-start = ((), (), s32[]{:S(2)}) async-start(), calls=%async_computation.12 | async-start | bytes 2621440 | tf_op jit(solution)/shard_map/all_gather | solution.py:39
  187.9 197.5 %all-reduce.9.cloned.1.call-start = ((), (), s32[]{:S(2)}) async-start(), calls=%async_computation.5 | async-start | bytes 1048576 | tf_op jit(solution)/shard_map/psum | solution.py:52
  348.9 114.9 %reduce-scatter.6.cloned.1.call-start = ((), (), s32[]{:S(2)}) async-start(), calls=%async_computation.6 | async-start | bytes 4128768 | tf_op jit(solution)/shard_map/reduce_scatter | solution.py:31
  400.1 7.6 copy-start.1
  417.0 75.9 %all-gather.12.cloned.1.call-start = ((), (), s32[]{:S(2)}) async-start(), calls=%async_computation.7 | async-start | bytes 2064384 | tf_op jit(solution)/shard_map/all_gather | solution.py:35
  465.5 81.8 %all-gather.18.cloned.1.call-start = ((), (), s32[]{:S(2)}) async-start(), calls=%async_computation.13 | async-start | bytes 2621440 | tf_op jit(solution)/shard_map/all_gather | solution.py:39
  501.5 197.7 %all-reduce.11.cloned.1.call-start = ((), (), s32[]{:S(2)}) async-start(), calls=%async_computation.8 | async-start | bytes 1048576 | tf_op jit(solution)/shard_map/psum | solution.py:52
  662.7 114.7 %reduce-scatter.8.cloned.1.call-start = ((), (), s32[]{:S(2)}) async-start(), calls=%async_computation.9 | async-start | bytes 4128768 | tf_op jit(solution)/shard_map/reduce_scatter | solution.py:31
  713.7 7.6 copy-start.2
  730.6 75.9 %all-gather.14.cloned.1.call-start = ((), (), s32[]{:S(2)}) async-start(), calls=%async_computation.10 | async-start | bytes 2064384 | tf_op jit(solution)/shard_map/all_gather | solution.py:35
  779.1 81.9 %all-gather.20.cloned.1.call-start = ((), (), s32[]{:S(2)}) async-start(), calls=%async_computation.14 | async-start | bytes 2621440 | tf_op jit(solution)/shard_map/all_gather | solution.py:39
  815.1 197.9 %all-reduce.13.cloned.1.call-start = ((), (), s32[]{:S(2)}) async-start(), calls=%async_computation.11 | async-start | bytes 1048576 | tf_op jit(solution)/shard_map/psum | solution.py:52
Sparse Core Ops, SparseCore 0:
  20.7 63.0 all-reduce.14
  102.3 47.7 reduce-scatter.3
  152.6 26.6 all-gather.9
  188.0 45.6 all-gather.15
  349.0 36.3 all-reduce.8
  417.1 46.5 reduce-scatter.5
  466.2 26.6 all-gather.11
  501.6 45.6 all-gather.17
  662.8 36.3 all-reduce.10
  730.7 46.5 reduce-scatter.7
  779.8 26.6 all-gather.13
  815.2 45.6 all-gather.19
  976.5 36.4 all-reduce.12
